TPU v7x, 32 devices: a whole 2x2x4 slice. The times are simulated.
32 devices in a mesh: panel: 4 (over y, x), tile: 8 (over z, core).
Axes of the slice: x: 2, y: 2, z: 4, core: 2. Of those that a mesh axis runs over, the one named last changes fastest.
Arguments:
- snapshots: bfloat16 [32, 64, 2, 512], P('panel', 'tile'), may hold values from -24 to 24
- beam_codes: int32 [32, 64], P(None, 'tile'), may hold values from 0 to 63
- panel_codes: int32 [32], replicated, may hold values from 0 to 63
- loading: float32 [32], P('panel'), may hold values from 1 to 10
Outputs:
- cancel: float32 [32, 62, 2], P('panel')
- beam_out: float32 [2, 512], P(None, 'tile')
All inputs are finite; a program needn't handle non-finite values.
Results may differ from a plain program's by a relative error of at most 0.0036.
Values may be sent and summed in bfloat16 or wider, within the bound.
A program may use at most 64 MiB of HBM per device.

v0:
```python
import functools
import math

import jax
import jax.numpy as jnp
from jax import lax
from jax.experimental import pallas as pl
from jax.experimental.pallas import tpu as pltpu
from jax.sharding import PartitionSpec as P

MESH = pl.DeviceIdType.MESH
LANES = 128
SUBS = 8
UNROLL1 = 2
UNROLL2 = 2
HIGH = lax.Precision.HIGHEST

phase_levels = 64
array_load = 1.0


def steering_rows(codes, total_tiles):
    angles = codes.astype(jnp.float32) * (2.0 * math.pi / phase_levels)
    cosine = jnp.cos(angles)
    sine = jnp.sin(angles)
    count_beams = codes.shape[0]
    count_tiles = codes.shape[1]
    real_rows = jnp.stack([cosine, sine], axis=-1).reshape(count_beams, 2 * count_tiles)
    imag_rows = jnp.stack([-sine, cosine], axis=-1).reshape(count_beams, 2 * count_tiles)
    table = jnp.stack([real_rows, imag_rows], axis=1).reshape(2 * count_beams, 2 * count_tiles)
    return (table / math.sqrt(total_tiles)).astype(jnp.bfloat16)


def solve_one(factor_one, right_one):
    return jax.scipy.linalg.cho_solve((factor_one, True), right_one)


def cancel_weights(covar):
    factor = jnp.linalg.cholesky(covar[:, 2:, 2:])
    return jax.vmap(solve_one)(factor, covar[:, 2:, :2])


def constraint_matrix(panel_codes):
    angles = panel_codes.astype(jnp.float32) * (2.0 * math.pi / phase_levels)
    cosine = jnp.cos(angles)
    sine = jnp.sin(angles)
    upper = jnp.stack([cosine, -sine], axis=-1)
    lower = jnp.stack([sine, cosine], axis=-1)
    return jnp.stack([upper, lower], axis=1).reshape(2 * panel_codes.shape[0], 2)


def array_weights(covar, constraint):
    factor = jnp.linalg.cholesky(covar)
    solved = jax.scipy.linalg.cho_solve((factor, True), constraint)
    gram = jnp.dot(constraint.T, solved, precision=HIGH)
    determinant = gram[0, 0] * gram[1, 1] - gram[0, 1] * gram[1, 0]
    inverse = (
        jnp.stack([jnp.stack([gram[1, 1], -gram[0, 1]]), jnp.stack([-gram[1, 0], gram[0, 0]])])
        / determinant
    )
    return jnp.dot(solved, inverse, precision=HIGH)


def plain_body(snapshots, beam_codes, panel_codes, loading):
    own_panels, own_tiles, _, snaps = snapshots.shape
    tile_count = lax.axis_size("tile")
    block_snaps = snaps // tile_count
    table = steering_rows(beam_codes, own_tiles * tile_count)
    samples = snapshots.reshape(own_panels, 2 * own_tiles, snaps)
    partial_value = jnp.einsum("bk,pks->pbs", table, samples, preferred_element_type=jnp.float32)
    totals = lax.psum(partial_value, "tile")
    summed = jnp.einsum("pis,pjs->pij", totals, totals, precision=HIGH)
    start = lax.axis_index("tile") * block_snaps
    beams = lax.dynamic_slice_in_dim(totals, start, block_snaps, 2)
    identity = jnp.eye(beams.shape[1], dtype=jnp.float32)
    covar = summed / snaps + loading[:, None, None] * identity[None, :, :]
    cancel = cancel_weights(covar)
    outputs = beams[:, :2, :] - jnp.einsum("pak,pas->pks", cancel, beams[:, 2:, :], precision=HIGH)
    gathered = lax.all_gather(outputs, "panel", axis=0, tiled=True)
    flat = gathered.reshape(gathered.shape[0] * 2, block_snaps)
    array_sum = lax.psum(jnp.dot(flat, flat.T, precision=HIGH), "tile")
    array_covar = array_sum / snaps + array_load * jnp.eye(flat.shape[0], dtype=jnp.float32)
    weights = array_weights(array_covar, constraint_matrix(panel_codes))
    beam_out = jnp.dot(weights.T, flat, precision=HIGH) * math.sqrt(flat.shape[0] // 2)
    return (cancel, beam_out)


def iota(shape, dim):
    return lax.broadcasted_iota(jnp.int32, shape, dim)


def cos_code(code):
    code = code & (phase_levels - 1)
    eighth = phase_levels // 8
    quarter = phase_levels // 4
    quadrant = ((code + eighth) >> 4) & 3
    rest = code - (((code + eighth) >> 4) * quarter)
    x = rest.astype(jnp.float32) * (2.0 * math.pi / phase_levels)
    y = x * x
    cosine = 1.0 + y * (-0.5 + y * (1 / 24 + y * (-1 / 720 + y * (1 / 40320 - y * (1 / 3628800)))))
    sine = x * (1.0 + y * (-1 / 6 + y * (1 / 120 + y * (-1 / 5040 + y * (1 / 362880)))))
    odd = (quadrant & 1) == 1
    flip = jnp.where((quadrant == 1) | (quadrant == 2), -1.0, 1.0)
    return jnp.where(odd, sine, cosine) * flip


def contract(a, b, dims, precision=HIGH):
    return lax.dot_general(a, b, (dims, ((), ())), precision=precision, preferred_element_type=jnp.float32)


def eliminate(rows, unroll):
    width = rows[0].shape[1]
    sub = iota((SUBS, width), 0)
    spread = lambda row: jnp.broadcast_to(row, (SUBS, width))

    def block(base, rows):
        def column(value, j):
            return jnp.take_along_axis(value, jnp.full((SUBS, width), base + j, jnp.int32), axis=1)

        group, others = rows[0], list(rows[1:])
        diag = [column(group, j) for j in range(SUBS)]
        factors = [[column(value, j) for value in others] for j in range(SUBS)]
        for j in range(SUBS):
            scale = 1.0 / spread(diag[j][j : j + 1])
            here = sub == j
            lead = diag[j] * scale

            def reduce(value):
                row = spread(value[j : j + 1])
                return jnp.where(here, row * scale, value - lead * row)

            for k in range(j + 1, SUBS):
                diag[k] = reduce(diag[k])
            group = reduce(group)
        spreads = [spread(group[j : j + 1]) for j in range(SUBS)]
        for r in range(len(others)):
            terms = [factors[j][r] * spreads[j] for j in range(SUBS)]
            while len(terms) > 1:
                terms = [sum(terms[i : i + 2][1:], terms[i]) for i in range(0, len(terms), 2)]
            others[r] = others[r] - terms[0]
        return others + [group]

    def step(index, rows):
        for u in range(unroll):
            rows = block((index * unroll + u) * SUBS, rows)
        return tuple(rows)

    steps = len(rows) // unroll
    if steps == 1:
        return list(step(0, rows))
    return list(lax.fori_loop(0, steps, step, tuple(rows)))


def fused_kernel(
    sizes, loading_in, snaps_in, codes_in, panel_codes_in, cancel_out, beam_out,
    loading, panel_codes, own, got, codes_own, codes_got, flat, cancels,
    local_sem, send_a, recv_a, send_c, recv_c, send_f, recv_f, send_w, recv_w,
):
    panel_count, tile_count, total_panels = sizes
    own_panels, own_tiles, _, snaps = snaps_in.shape
    total_tiles = own_tiles * tile_count
    beams_count = codes_in.shape[1]
    width = 2 * beams_count
    chunks = snaps // LANES
    pi, ti = lax.axis_index("panel"), lax.axis_index("tile")
    devices = panel_count * tile_count

    peers = []
    for dp in range(panel_count):
        for dt in range(tile_count):
            if dp or dt:
                peers.append((dp, dt))
    there = lambda dp, dt: (lax.rem(pi + dp, panel_count), lax.rem(ti + dt, tile_count))
    back = lambda dp, dt: (
        lax.rem(pi + panel_count - dp, panel_count),
        lax.rem(ti + tile_count - dt, tile_count),
    )

    barrier = pltpu.get_barrier_semaphore()
    near = [(dp, dt) for dp, dt in peers if not (dp and dt)]
    for dp, dt in near:
        pl.semaphore_signal(barrier, inc=1, device_id=there(dp, dt), device_id_type=MESH)
    loads = [
        pltpu.make_async_copy(source, target, local_sem.at[index])
        for index, (source, target) in enumerate((
            (codes_in, codes_own),
            (snaps_in, own),
            (snaps_in.at[ti], got.at[ti]),
            (codes_in, codes_got.at[ti]),
            (loading_in, loading),
            (panel_codes_in, panel_codes),
        ))
    ]
    for load in loads:
        load.start()
    for load in loads:
        load.wait()
    pl.semaphore_wait(barrier, len(near))

    waits = []
    for dt in list(range(1, tile_count)):
        to = there(0, dt)
        source = back(0, dt)[1]
        piece = pltpu.make_async_remote_copy(
            codes_own, codes_got.at[ti], send_c.at[dt], recv_c.at[ti], device_id=to, device_id_type=MESH
        )
        piece.start()
        arrival = pltpu.make_async_remote_copy(
            codes_own, codes_got.at[source], send_c.at[dt], recv_c.at[source], device_id=to, device_id_type=MESH
        )
        waits.append((piece, arrival))
    bulk = []
    for dt in list(range(1, tile_count)):
        to = there(0, dt)
        source = back(0, dt)[1]
        piece = pltpu.make_async_remote_copy(
            own.at[to[1]], got.at[ti], send_a.at[dt], recv_a.at[ti], device_id=to, device_id_type=MESH
        )
        piece.start()
        arrival = pltpu.make_async_remote_copy(
            own.at[to[1]], got.at[source], send_a.at[dt], recv_a.at[source], device_id=to, device_id_type=MESH
        )
        bulk.append((piece, arrival))

    order = 2 * total_panels
    code_row = jnp.broadcast_to(panel_codes[...], (order, total_panels))
    own_code = jnp.where(iota((order, total_panels), 1) == lax.rem(iota((order, total_panels), 0), total_panels), code_row, 0)
    code_col = jnp.broadcast_to(jnp.sum(own_code, axis=1, keepdims=True), (order, LANES))
    lower = iota((order, LANES), 0) >= total_panels
    lane = iota((order, LANES), 1)
    quarter = phase_levels // 4
    shift = jnp.where(lane == 0, jnp.where(lower, -quarter, 0), jnp.where(lower, 0, quarter))
    constraint = jnp.where(lane < 2, cos_code(code_col + shift), 0.0)

    for piece, arrival in waits:
        piece.wait_send()
        arrival.wait_recv()
    codes_all = codes_got[...].reshape(total_tiles, beams_count).astype(jnp.float32)
    k_rows = (iota((2 * total_tiles, total_tiles), 0) >> 1) == iota((2 * total_tiles, total_tiles), 1)
    beam_of = lambda index: lax.rem(index + 2, width)
    b_cols = (beam_of(iota((beams_count, width), 1)) >> 1) == iota((beams_count, width), 0)
    tall = contract(k_rows.astype(jnp.bfloat16), codes_all.astype(jnp.bfloat16), ((1,), (0,)), None)
    wide = contract(tall.astype(jnp.bfloat16), b_cols.astype(jnp.bfloat16), ((1,), (0,)), None)
    code = (wide + 0.5).astype(jnp.int32)
    k_odd = iota(code.shape, 0) & 1
    i_odd = iota(code.shape, 1) & 1
    table = cos_code(code + quarter * (i_odd - k_odd)) / math.sqrt(total_tiles)
    table = table.astype(jnp.bfloat16)

    for piece, arrival in bulk:
        piece.wait_send()
        arrival.wait_recv()
    samples = got[...].reshape(2 * total_tiles, snaps)
    beams = contract(table, samples, ((0,), (0,)), None)
    covar = contract(beams, beams, ((1,), (1,))) / snaps
    diagonal = iota((width, width), 0) == iota((width, width), 1)
    covar = covar + jnp.where(diagonal, loading[ti], 0.0)
    row, col = iota((width, width), 0), iota((width, width), 1)
    inside = (row < width - 2) & (col < width - 2)
    full = jnp.concatenate([jnp.where(inside, covar, jnp.where(diagonal, 1.0, 0.0)), covar], axis=1)
    groups = eliminate([full[r : r + SUBS] for r in range(0, width, SUBS)], UNROLL1)
    solved = jnp.concatenate(groups, axis=0)[:, width:]
    mix = jnp.where(iota((width, width), 0) < width - 2, -solved, jnp.where(diagonal, 1.0, 0.0))
    outputs = contract(mix, beams, ((0,), (0,)))
    own_panel = pi * own_panels + ti
    for j in range(chunks):
        flat[own_panel, 2 * j : 2 * j + 2, :] = outputs[width - 2 :, j * LANES : (j + 1) * LANES]

    arrivals = []
    for dp, dt in peers:
        to = there(dp, dt)
        source = back(dp, dt)
        slot = source[0] * own_panels + source[1]
        piece = pltpu.make_async_remote_copy(
            flat.at[own_panel], flat.at[own_panel], send_f.at[dp * tile_count + dt], recv_f.at[own_panel],
            device_id=to, device_id_type=MESH,
        )
        piece.start()
        arrival = pltpu.make_async_remote_copy(
            flat.at[slot], flat.at[slot], send_f.at[dp * tile_count + dt], recv_f.at[slot],
            device_id=to, device_id_type=MESH,
        )
        arrivals.append((piece, arrival))
    side = mix.T[width - 2 :, :]
    cancels[ti, :, :width] = -side
    passes = []
    for dt in range(1, tile_count):
        to = there(0, dt)
        source = back(0, dt)[1]
        piece = pltpu.make_async_remote_copy(
            cancels.at[ti], cancels.at[ti], send_w.at[dt], recv_w.at[ti], device_id=to, device_id_type=MESH
        )
        piece.start()
        arrival = pltpu.make_async_remote_copy(
            cancels.at[source], cancels.at[source], send_w.at[dt], recv_w.at[source], device_id=to, device_id_type=MESH
        )
        passes.append((piece, arrival))

    for piece, arrival in arrivals:
        piece.wait_send()
        arrival.wait_recv()
    pick = lambda row: flat[:, pl.ds(row, 1), :].reshape(total_panels, LANES)
    parts = [jnp.concatenate([flat[:, 2 * j, :], flat[:, 2 * j + 1, :]], axis=0) for j in range(chunks)]
    array_covar = contract(parts[0], parts[0], ((1,), (1,)))
    for part in parts[1:]:
        array_covar = array_covar + contract(part, part, ((1,), (1,)))
    eye = jnp.where(iota((order, order), 0) == iota((order, order), 1), array_load, 0.0)
    array_covar = array_covar / snaps + eye
    full = jnp.concatenate([array_covar, constraint[:, : LANES - order]], axis=1)
    groups = eliminate([full[r : r + SUBS] for r in range(0, order, SUBS)], UNROLL2)
    solved = jnp.concatenate(groups, axis=0)[:, order:]
    block = snaps // tile_count
    per = LANES // block
    chunk = ti // per
    mine = parts[0]
    for j in range(1, chunks):
        mine = jnp.where(chunk == j, parts[j], mine)
    joint = contract(solved, jnp.concatenate([mine, constraint], axis=1), ((0,), (0,)))[:SUBS]
    gram_t = joint[:, LANES : LANES + 2]
    g00, g01 = gram_t[0:1, 0:1], gram_t[1:2, 0:1]
    g10, g11 = gram_t[0:1, 1:2], gram_t[1:2, 1:2]
    scale = math.sqrt(total_panels) / (g00 * g11 - g01 * g10)
    s0, s1 = joint[0:1, :LANES], joint[1:2, :LANES]
    row0 = (g11 * s0 - g10 * s1) * scale
    row1 = (g00 * s1 - g01 * s0) * scale
    both = jnp.concatenate([row0, row1], axis=0)
    spot = lax.rem(ti, per)
    chosen = both[:, :block]
    for j in range(1, per):
        chosen = jnp.where(spot == j, both[:, j * block : (j + 1) * block], chosen)
    beam_out[...] = chosen

    for piece, arrival in passes:
        piece.wait_send()
        arrival.wait_recv()
    cancel_out[...] = cancels[:, :, : width - 2]


def fused_body(panel_count, tile_count, snapshots, beam_codes, panel_codes, loading):
    own_panels, own_tiles, _, snaps = snapshots.shape
    beams_count = beam_codes.shape[0]
    total_panels = own_panels * panel_count
    dma = pltpu.SemaphoreType.DMA
    devices = panel_count * tile_count
    any_space = pl.BlockSpec(memory_space=pl.ANY)
    vmem = pl.BlockSpec(memory_space=pltpu.VMEM)
    cancel_t, beam_out = pl.pallas_call(
        functools.partial(fused_kernel, (panel_count, tile_count, total_panels)),
        out_shape=(
            pltpu.VMEM((own_panels, 2, 2 * beams_count - 2), jnp.float32),
            pltpu.VMEM((2, snaps // tile_count), jnp.float32),
        ),
        in_specs=[any_space] * 4,
        out_specs=(vmem, vmem),
        scratch_shapes=[
            pltpu.SMEM(loading.shape, loading.dtype),
            pltpu.VMEM((1, total_panels), jnp.int32),
            pltpu.VMEM(snapshots.shape, snapshots.dtype),
            pltpu.VMEM((tile_count, own_tiles, 2, snaps), snapshots.dtype),
            pltpu.VMEM((own_tiles, beams_count), jnp.int32),
            pltpu.VMEM((tile_count, own_tiles, beams_count), jnp.int32),
            pltpu.VMEM((total_panels, 2 * snaps // LANES, LANES), jnp.float32),
            pltpu.VMEM((own_panels, 2, LANES), jnp.float32),
            dma((6,)),
            dma((tile_count,)),
            dma((tile_count,)),
            dma((tile_count,)),
            dma((tile_count,)),
            dma((devices,)),
            dma((total_panels,)),
            dma((tile_count,)),
            dma((tile_count,)),
        ],
        compiler_params=pltpu.CompilerParams(collective_id=0, has_side_effects=True),
        name="beamformer",
    )(loading, snapshots, beam_codes.T, panel_codes.reshape(1, -1))
    return (jnp.transpose(cancel_t, (0, 2, 1)), beam_out)


def body(mesh_shape, snapshots, beam_codes, panel_codes, loading):
    panel_count, tile_count = mesh_shape
    own_panels, own_tiles, _, snaps = snapshots.shape
    block = snaps // tile_count
    fits = (
        own_panels == tile_count
        and own_tiles % SUBS == 0
        and 4 * beam_codes.shape[0] == LANES
        and (2 * own_panels * panel_count) % SUBS == 0
        and 2 * own_panels * panel_count + 2 <= LANES
        and 2 * snaps == SUBS * LANES
        and block <= LANES
        and LANES % block == 0
    )
    if not fits:
        return plain_body(snapshots, beam_codes, panel_codes, loading)
    return fused_body(panel_count, tile_count, snapshots, beam_codes, panel_codes, loading)


def solution(mesh):
    placed = (P("panel", "tile", None, None), P(None, "tile"), P(), P("panel"))
    return jax.shard_map(
        functools.partial(body, (mesh.shape["panel"], mesh.shape["tile"])),
        mesh=mesh,
        in_specs=placed,
        out_specs=(P("panel", None, None), P(None, "tile")),
        check_vma=False,
    )
```

profile of v0, /device:TPU:0, one launch (start us, length us, event | category | flops | bytes accessed | tf_op | source)
XLA Modules:
  0.0 24.3 jit_solution(7988763766226972532)
XLA Ops:
  0.6 22.5 %beamformer.1 = (f32[8,2,62]{2,1,0:T(2,128)S(1)}, f32[2,64]{1,0:T(2,128)S(1)}) custom-call(f32[8]{0:T(128)} %loading_in.1, bf16[8,8,2,512]{3,2,1,0:T(2,128)(2,1)} %snaps_in.1, s32[8,32]{1,0:T(8,128)} %bitcast.4, s32[1,32]{1,0:T(1,128)} %bitcast.5), custom_call_target="tpu_custom_call" | custom-call | tf_op jit(solution)/shard_map/beamformer/pallas_call | solution.py:347
  23.1 0.6 %copy.8 = f32[8,62,2]{1,2,0:T(2,128)} copy(f32[8,62,2]{1,2,0:T(2,128)S(1)} %bitcast.3) | data formatting | bytes 7936
  23.7 0.6 %copy.9 = f32[2,64]{1,0:T(2,128)} copy(f32[2,64]{1,0:T(2,128)S(1)} %get-tuple-element.7) | data formatting | bytes 1024
where the time goes:
time: 24.5 us; the launch traced here: 24.3 us
  Pallas kernels  22.5 us (92%)
  local copies, waits for them, and re-layouts  1.16 us (5%)
  between operations  0.64 us (3%)
    pallas_call x1, Pallas kernels, fused_body(): pl.pallas_call(functools.partial(fused_kernel, (panel_count, tile_count,...  22.5 us
    unnamed x2, local copies, waits for them, and re-layouts  1.16 us

commit v1 on v0

--- a/solution.py
+++ b/solution.py
@@ -108,6 +108,16 @@
     return lax.dot_general(a, b, (dims, ((), ())), precision=precision, preferred_element_type=jnp.float32)
 
 
+def far_first(own, count):
+    order = []
+    for k in range(count - 1):
+        down = count - 1 - k
+        down = jnp.where(down <= own, down - 1, down)
+        up = jnp.where(k >= own, k + 1, k)
+        order.append(jnp.where(own < count // 2, down, up))
+    return order
+
+
 def eliminate(rows, unroll):
     width = rows[0].shape[1]
     sub = iota((SUBS, width), 0)
@@ -197,28 +207,26 @@
         load.wait()
     pl.semaphore_wait(barrier, len(near))
 
+    tiles = far_first(ti, tile_count)
+    panels = far_first(pi, panel_count)
     waits = []
-    for dt in list(range(1, tile_count)):
-        to = there(0, dt)
-        source = back(0, dt)[1]
+    for k, other in enumerate(tiles, 1):
         piece = pltpu.make_async_remote_copy(
-            codes_own, codes_got.at[ti], send_c.at[dt], recv_c.at[ti], device_id=to, device_id_type=MESH
+            codes_own, codes_got.at[ti], send_c.at[k], recv_c.at[ti], device_id=(pi, other), device_id_type=MESH
         )
         piece.start()
         arrival = pltpu.make_async_remote_copy(
-            codes_own, codes_got.at[source], send_c.at[dt], recv_c.at[source], device_id=to, device_id_type=MESH
+            codes_own, codes_got.at[other], send_c.at[k], recv_c.at[other], device_id=(pi, other), device_id_type=MESH
         )
         waits.append((piece, arrival))
     bulk = []
-    for dt in list(range(1, tile_count)):
-        to = there(0, dt)
-        source = back(0, dt)[1]
+    for k, other in enumerate(tiles, 1):
         piece = pltpu.make_async_remote_copy(
-            own.at[to[1]], got.at[ti], send_a.at[dt], recv_a.at[ti], device_id=to, device_id_type=MESH
+            own.at[other], got.at[ti], send_a.at[k], recv_a.at[ti], device_id=(pi, other), device_id_type=MESH
         )
         piece.start()
         arrival = pltpu.make_async_remote_copy(
-            own.at[to[1]], got.at[source], send_a.at[dt], recv_a.at[source], device_id=to, device_id_type=MESH
+            own.at[other], got.at[other], send_a.at[k], recv_a.at[other], device_id=(pi, other), device_id_type=MESH
         )
         bulk.append((piece, arrival))
 
@@ -233,7 +241,6 @@
     constraint = jnp.where(lane < 2, cos_code(code_col + shift), 0.0)
 
     for piece, arrival in waits:
-        piece.wait_send()
         arrival.wait_recv()
     codes_all = codes_got[...].reshape(total_tiles, beams_count).astype(jnp.float32)
     k_rows = (iota((2 * total_tiles, total_tiles), 0) >> 1) == iota((2 * total_tiles, total_tiles), 1)
@@ -248,7 +255,6 @@
     table = table.astype(jnp.bfloat16)
 
     for piece, arrival in bulk:
-        piece.wait_send()
         arrival.wait_recv()
     samples = got[...].reshape(2 * total_tiles, snaps)
     beams = contract(table, samples, ((0,), (0,)), None)
@@ -267,17 +273,16 @@
         flat[own_panel, 2 * j : 2 * j + 2, :] = outputs[width - 2 :, j * LANES : (j + 1) * LANES]
 
     arrivals = []
-    for dp, dt in peers:
-        to = there(dp, dt)
-        source = back(dp, dt)
-        slot = source[0] * own_panels + source[1]
+    targets = [(p, t) for t in tiles for p in panels + [pi]] + [(p, ti) for p in panels]
+    for k, to in enumerate(targets):
+        slot = to[0] * own_panels + to[1]
         piece = pltpu.make_async_remote_copy(
-            flat.at[own_panel], flat.at[own_panel], send_f.at[dp * tile_count + dt], recv_f.at[own_panel],
+            flat.at[own_panel], flat.at[own_panel], send_f.at[k], recv_f.at[own_panel],
             device_id=to, device_id_type=MESH,
         )
         piece.start()
         arrival = pltpu.make_async_remote_copy(
-            flat.at[slot], flat.at[slot], send_f.at[dp * tile_count + dt], recv_f.at[slot],
+            flat.at[slot], flat.at[slot], send_f.at[k], recv_f.at[slot],
             device_id=to, device_id_type=MESH,
         )
         arrivals.append((piece, arrival))
@@ -297,7 +302,6 @@
         passes.append((piece, arrival))
 
     for piece, arrival in arrivals:
-        piece.wait_send()
         arrival.wait_recv()
     pick = lambda row: flat[:, pl.ds(row, 1), :].reshape(total_panels, LANES)
     parts = [jnp.concatenate([flat[:, 2 * j, :], flat[:, 2 * j + 1, :]], axis=0) for j in range(chunks)]
@@ -331,8 +335,9 @@
     beam_out[...] = chosen
 
     for piece, arrival in passes:
+        arrival.wait_recv()
+    for piece, arrival in waits + bulk + arrivals + passes:
         piece.wait_send()
-        arrival.wait_recv()
     cancel_out[...] = cancels[:, :, : width - 2]
 
 

time: 24.5 us -> 23.9 us (0.976); the launches traced: 24.3 us -> 23.4 us
  Pallas kernels: 22.5 us -> 21.6 us
    pallas_call x1, Pallas kernels: 22.5 us -> 21.6 us  [fused_body(): pl.pallas_call(functools.partial(fused_kernel, (panel_count, tile_count,...]
where the time goes in v1:
time: 23.9 us; the launch traced here: 23.4 us
  Pallas kernels  21.6 us (90%)
  local copies, waits for them, and re-layouts  1.16 us (5%)
  between operations  0.64 us (3%)
    pallas_call x1, Pallas kernels, fused_body(): pl.pallas_call(functools.partial(fused_kernel, (panel_count, tile_count,...  21.6 us
    unnamed x2, local copies, waits for them, and re-layouts  1.16 us

profile of v1, /device:TPU:0, one launch (start us, length us, event | category | flops | bytes accessed | tf_op | source)
XLA Modules:
  0.0 23.4 jit_solution(13983183894450633722)
XLA Ops:
  0.6 21.6 %beamformer.1 = (f32[8,2,62]{2,1,0:T(2,128)S(1)}, f32[2,64]{1,0:T(2,128)S(1)}) custom-call(f32[8]{0:T(128)} %loading_in.1, bf16[8,8,2,512]{3,2,1,0:T(2,128)(2,1)} %snaps_in.1, s32[8,32]{1,0:T(8,128)} %bitcast.4, s32[1,32]{1,0:T(1,128)} %bitcast.5), custom_call_target="tpu_custom_call" | custom-call | tf_op jit(solution)/shard_map/beamformer/pallas_call | solution.py:352
  22.2 0.6 %copy.8 = f32[8,62,2]{1,2,0:T(2,128)} copy(f32[8,62,2]{1,2,0:T(2,128)S(1)} %bitcast.3) | data formatting | bytes 7936
  22.8 0.6 %copy.9 = f32[2,64]{1,0:T(2,128)} copy(f32[2,64]{1,0:T(2,128)S(1)} %get-tuple-element.7) | data formatting | bytes 1024
